TPU v7x, 32 devices: a whole 2x2x4 slice. The times are simulated.
32 devices in a mesh: rep: 2 (over y), gx: 16 (over z, x, core).
Axes of the slice: x: 2, y: 2, z: 4, core: 2. Of those that a mesh axis runs over, the one named last changes fastest.
Arguments:
- positions: float32 [3, 49152], P(None, ('rep', 'gx')), parts along dimension 1, may hold values from 0 to 96
- velocities: float32 [3, 49152], P(None, ('rep', 'gx')), parts along dimension 1, may hold values from -9 to 9
- atom_params: float32 [4, 49152], P(None, ('rep', 'gx')), parts along dimension 1, may hold values from -1 to 2, as said below
- pair_list: int32 [3, 540672], P(None, ('rep', 'gx')), parts along dimension 1, may hold values from 0 to 479, as said below
- pair_count: int32 [32], P(('rep', 'gx')), parts along dimension 0, may hold values from 2112 to 16896, as said below
- exclusion: int32 [4, 540672], P(None, ('rep', 'gx')), parts along dimension 1, may hold values from 0 to 65535, as said below
- halo_far: int32 [3072], P(('rep', 'gx')), parts along dimension 0, may hold values from 0 to 191, as said below
- box_lengths: float32 [6], P('rep'), parts along dimension 0, may hold values from 12 to 96
- extended_variables: float32 [8], P('rep'), parts along dimension 0, may hold values from -0.3 to 0.3
Outputs:
- forces: float32 [3, 49152], P(None, ('rep', 'gx')), parts along dimension 1
- new_velocities: float32 [3, 49152], P(None, ('rep', 'gx')), parts along dimension 1
- new_positions: float32 [3, 49152], P(None, ('rep', 'gx')), parts along dimension 1
- new_coupling: float32 [8], P('rep'), parts along dimension 0
There are 2 independent parts, one for each index of `rep`. A program takes and returns all parts, laid end to end along the dimension named above; each array names one. Nothing has to cross between parts.
Inputs may be any that keep to these rules, and one draw needn't show every extreme that they name: `pair_list`: row 0 is a local cluster 0 to 191, row 1 a slot 0 to 479 of the slot table, row 2 an image code 0 to 8. Over each domain's used columns row 0 never falls (the list is grouped by its first cluster). Unused columns hold valid entries too. `pair_count`: at most 16896; some domain uses all 16896 columns in every draw. `exclusion`: each word holds 16 bits; bit 1 means the atom pair interacts. `halo_far`: 96 distinct local clusters of each domain. `atom_params`: rows 1 to 3 are positive.
All inputs are finite; a program needn't handle non-finite values.
Results may differ from a plain program's by a relative error of at most 0.0003.
Values sent between devices are 32-bit elements; how exact they have to be, the bound alone decides.
A program may use at most 64 MiB of HBM per device.

v0:
```python
import jax
import jax.numpy as jnp
from jax import lax
from jax.sharding import PartitionSpec as P

LY = 12
time_step = 0.25
reaction_term = 1.0 / 1331.0
thermal_scale_unit = 2.0
reservoir_inertia_mass = 4.0
barostat_gain = 0.1
pressure_target = 1.0


def passed_along(value, axis, steps):
    count = lax.axis_size(axis)
    pairs = [(source, (source + steps) % count) for source in range(count)]
    return lax.ppermute(value, axis, pairs)


def pair_tiles(slot_table, pair_rows, word_rows, usable, box_lengths):
    tile_width = pair_rows.shape[1]
    first_rows = jnp.take(slot_table, pair_rows[0], axis=0).T.reshape(6, 8, tile_width)
    second_rows = jnp.take(slot_table, pair_rows[1], axis=0).T.reshape(6, 8, tile_width)
    image_y = (pair_rows[2] // 3 - 1).astype(jnp.float32) * box_lengths[1]
    image_z = (pair_rows[2] % 3 - 1).astype(jnp.float32) * box_lengths[2]
    delta_x = second_rows[0][None, :, :] - first_rows[0][:, None, :]
    delta_y = second_rows[1][None, :, :] - first_rows[1][:, None, :] + image_y
    delta_z = second_rows[2][None, :, :] - first_rows[2][:, None, :] + image_z
    shifts = (jnp.arange(64, dtype=jnp.int32) % 16)[:, None]
    mask_bits = jnp.right_shift(jnp.repeat(word_rows, 16, axis=0), shifts) & 1
    interact = (mask_bits.reshape(8, 8, tile_width) == 1) & usable[None, None, :]
    radius_sq = delta_x * delta_x + delta_y * delta_y + delta_z * delta_z
    radius_sq = jnp.where(interact, radius_sq, 1.0)
    inverse = lax.rsqrt(radius_sq)
    inverse_sq = inverse * inverse
    inverse_six = inverse_sq * inverse_sq * inverse_sq
    charge_pair = first_rows[3][:, None, :] * second_rows[3][None, :, :]
    dispersion = first_rows[4][:, None, :] * second_rows[4][None, :, :]
    repulsion = first_rows[5][:, None, :] * second_rows[5][None, :, :]
    scalar = (
        charge_pair * (inverse * inverse_sq - reaction_term)
        + (12.0 * repulsion * inverse_six - 6.0 * dispersion) * inverse_six * inverse_sq
    )
    scalar = jnp.where(interact, scalar, 0.0)
    components = (delta_x, delta_y, delta_z)
    onto_second = jnp.stack([jnp.sum(scalar * component, axis=0) for component in components])
    onto_first = -jnp.stack([jnp.sum(scalar * component, axis=1) for component in components])
    virial = -0.5 * jnp.stack([jnp.sum(scalar * component * component) for component in components])
    tile_terms = jnp.concatenate(
        [onto_first.reshape(24, tile_width), onto_second.reshape(24, tile_width)], axis=1
    ).T
    owners = jnp.concatenate([pair_rows[0], pair_rows[1]])
    return (tile_terms, owners, virial)


def on_device(
    positions,
    velocities,
    atom_params,
    pair_list,
    pair_count,
    exclusion,
    halo_far,
    box_lengths,
    extended_variables,
):
    atoms_here = positions.shape[1]
    clusters = atoms_here // 8
    far_clusters = halo_far.shape[0]
    slots = 2 * clusters + far_clusters
    block_rows = pair_list.shape[1] // LY
    domain_index = lax.axis_index("gx")
    axis_count = lax.axis_size("gx")
    inverse_mass = atom_params[3]
    kinetic = 0.5 * jnp.sum(velocities * velocities / inverse_mass[None, :], axis=1)
    overall_motion_work = lax.psum(kinetic, "gx")
    packed = jnp.concatenate([positions, atom_params[:3]], axis=0)
    far_rows = packed.reshape(6, clusters, 8)[:, halo_far, :].reshape(6, far_clusters * 8)
    near_rows = passed_along(packed, "gx", -1)
    far_in = passed_along(far_rows, "gx", -2)
    near_rows = near_rows.at[0].add(jnp.where(domain_index == axis_count - 1, box_lengths[0], 0.0))
    far_in = far_in.at[0].add(jnp.where(domain_index >= axis_count - 2, box_lengths[0], 0.0))
    slot_table = jnp.concatenate([packed, near_rows, far_in], axis=1)
    slot_table = slot_table.reshape(6, slots, 8).transpose(1, 0, 2).reshape(slots, 48)
    pair_total = pair_count[0]
    slot_numbers = jnp.arange(slots, dtype=jnp.int32)[:, None]

    def one_block(block_index, running):
        accumulated, virial = running
        first_row = block_index * block_rows
        pair_block = lax.dynamic_slice_in_dim(pair_list, first_row, block_rows, 1)
        word_block = lax.dynamic_slice_in_dim(exclusion, first_row, block_rows, 1)
        usable = first_row + jnp.arange(block_rows, dtype=jnp.int32) < pair_total
        tile_terms, owners, partial_value = pair_tiles(
            slot_table, pair_block, word_block, usable, box_lengths
        )
        selector = (slot_numbers == owners[None, :]).astype(jnp.float32)
        accumulated = accumulated + jnp.dot(
            selector,
            tile_terms,
            precision=lax.Precision.HIGHEST,
            preferred_element_type=jnp.float32,
        )
        return (accumulated, virial + partial_value)

    block_count = (pair_total + block_rows - 1) // block_rows
    start_state = (jnp.zeros((slots, 24), jnp.float32), jnp.zeros((3,), jnp.float32))
    accumulated, virial = lax.fori_loop(0, block_count, one_block, start_state)
    columns = accumulated.T
    near_back = passed_along(columns[:, clusters : 2 * clusters], "gx", 1)
    far_back = passed_along(columns[:, 2 * clusters :], "gx", 2)
    summed = columns[:, :clusters] + near_back
    summed = summed.at[:, halo_far].add(far_back)
    forces = summed.reshape(3, 8, clusters).transpose(0, 2, 1).reshape(3, atoms_here)
    virial_total = lax.psum(virial, "gx")
    combined_potential = jnp.sum(overall_motion_work)
    particle_number_overall = atoms_here * axis_count
    volume = box_lengths[0] * box_lengths[1] * box_lengths[2]
    thermal_ratio_value = (
        2.0 * combined_potential / (3.0 * particle_number_overall * thermal_scale_unit)
    )
    reservoir_damping = extended_variables[0] + reservoir_inertia_mass * (thermal_ratio_value - 1.0)
    box_rates = extended_variables[1:] + barostat_gain * (
        overall_motion_work - virial_total - pressure_target * volume / 2.0
    ) / (combined_potential / 3.0)
    new_velocities = velocities + time_step * (
        forces * inverse_mass[None, :] - (reservoir_damping + box_rates[:, None]) * velocities
    )
    new_positions = positions * (1.0 + time_step * box_rates[:, None]) + time_step * new_velocities
    new_coupling = jnp.concatenate([reservoir_damping[None], box_rates])
    return (forces, new_velocities, new_positions, new_coupling)


def solution(mesh):
    return jax.shard_map(
        on_device,
        mesh=mesh,
        in_specs=(
            P(None, ("rep", "gx")),
            P(None, ("rep", "gx")),
            P(None, ("rep", "gx")),
            P(None, ("rep", "gx")),
            P(("rep", "gx")),
            P(None, ("rep", "gx")),
            P(("rep", "gx")),
            P("rep"),
            P("rep"),
        ),
        out_specs=(
            P(None, ("rep", "gx")),
            P(None, ("rep", "gx")),
            P(None, ("rep", "gx")),
            P("rep"),
        ),
        check_vma=False,
    )
```

profile of v0, /device:TPU:0, one launch (start us, length us, event | category | flops | bytes accessed | tf_op | source)
XLA Modules:
  0.0 471.5 jit_solution(7879650573326393458)
XLA Ops:
  1.4 5.5 %collective-permute-start = (f32[6,1536]{1,0:T(8,128)S(1)}, f32[6,1536]{1,0:T(8,128)S(1)}, u32[]{:S(2)}, u32[]{:S(2)}) collective-permute-start(f32[6,1536]{1,0:T(8,128)S(1)} %pad_maximum_fusion.1), channel_id=1, source_target_pairs={{0,15},{1,0},{2,1},{3,2},{4,3},{5,4},{6,5},{7,6},{8,7},{9,8},{10,9... | collective-permute-start | bytes 110600 | tf_op jit(solution)/shard_map/ppermute | solution.py:18
  18.8 408.7 %while.18 = (s32[]{:T(128)}, f32[480,24]{0,1:T(8,128)}, f32[3]{0:T(128)}, s32[]{:T(128)}, s32[3,16896]{1,0:T(4,128)}, /*index=5*/s32[4,16896]{1,0:T(4,128)}, s32...) while((s32[]{:T(128)}, f32[480,24]{0,1:T(8,128)}, ...), condition=%wide.region_10.12_spmd.clone, body=%wide.region_0.11_spmd.clone.sunk | while | flops 397501280 | bytes 8990699 | solution.py:109
  26.0 2.7 gather_fusion.1
  29.0 2.7 gather_fusion
  60.0 2.7 gather_fusion.1
  63.0 2.7 gather_fusion
  94.2 2.7 gather_fusion.1
  97.1 2.7 gather_fusion
  128.2 2.7 gather_fusion.1
  131.2 2.7 gather_fusion
  151.9 2.5 fusion.65
  162.3 2.7 gather_fusion.1
  165.2 2.7 gather_fusion
  186.0 2.5 fusion.65
  196.4 2.7 gather_fusion.1
  199.3 2.7 gather_fusion
  220.0 2.5 fusion.65
  230.4 2.7 gather_fusion.1
  233.4 2.7 gather_fusion
  264.5 2.7 gather_fusion.1
  267.4 2.7 gather_fusion
  298.5 2.7 gather_fusion.1
  301.5 2.7 gather_fusion
  322.2 2.5 fusion.65
  332.6 2.7 gather_fusion.1
  335.5 2.7 gather_fusion
  366.6 2.7 gather_fusion.1
  369.6 2.7 gather_fusion
  400.7 2.7 gather_fusion.1
  403.6 2.7 gather_fusion
  427.5 29.8 %all-reduce = (f32[3]{0:T(128)S(1)}, f32[3]{0:T(128)S(1)}) all-reduce(f32[3]{0:T(128)} %broadcast_multiply_fusion, f32[3]{0:T(128)} %get-tuple-element.496), channel_id=1, replica_groups=mesh['rep'=2,'gx'=16] {'gx'}, use_global_device_ids=true, to_apply=%region_13.15 | all-reduce | flops 6 | bytes 48 | tf_op jit(solution)/shard_map/psum | solution.py:77
  462.3 4.7 %collective-permute-done.2 = f32[24,192]{0,1:T(8,128)S(1)} collective-permute-done((f32[24,192]{0,1:T(8,128)S(1)}, f32[24,192]{0,1:T(8,128)S(1)}, u32[]{:S(2)}, u32[]{:S(2)}) %collective-permute-start.2) | collective-permute-done | bytes 18464 | tf_op jit(solution)/shard_map/ppermute | solution.py:18
  (777 shorter events, 347.8 us)
Async XLA Ops:
  1.4 14.6 %collective-permute-start = (f32[6,1536]{1,0:T(8,128)S(1)}, f32[6,1536]{1,0:T(8,128)S(1)}, u32[]{:S(2)}, u32[]{:S(2)}) collective-permute-start(f32[6,1536]{1,0:T(8,128)S(1)} %pad_maximum_fusion.1), channel_id=1, source_target_pairs={{0,15},{1,0},{2,1},{3,2},{4,3},{5,4},{6,5},{7,6},{8,7},{9,8},{10,9... | collective-permute-start | bytes 110600 | tf_op jit(solution)/shard_map/ppermute | solution.py:18
  8.5 7.7 %copy-start.4 = (f32[3,1536]{1,0:T(4,128)S(1)}, f32[3,1536]{1,0:T(4,128)}, u32[]{:S(2)}) copy-start(f32[3,1536]{1,0:T(4,128)} %param.17) | copy-start | bytes 55300
  9.8 6.0 %collective-permute-start.1 = (f32[6,768]{1,0:T(8,128)S(1)}, f32[6,768]{1,0:T(8,128)S(1)}, u32[]{:S(2)}, u32[]{:S(2)}) collective-permute-start(f32[6,768]{1,0:T(8,128)S(1)} %reshape.315), channel_id=1, source_target_pairs={{0,14},{1,15},{2,0},{3,1},{4,2},{5,3},{6,4},{7,5},{8,6},{9,7},{10,... | collective-permute-start | bytes 55304 | tf_op jit(solution)/shard_map/ppermute | solution.py:18
  10.5 5.5 %copy-start.15 = (f32[1536]{0:T(1024)}, f32[1536]{0:T(1024)S(1)}, u32[]{:S(2)}) copy-start(f32[1536]{0:T(1024)S(1)} %slice_reduce_fusion) | copy-start | bytes 18436
  45.7 4.0 copy-start.7
  46.4 6.4 %copy-start.14 = (f32[3]{0:T(128)S(1)}, f32[3]{0:T(128)}, u32[]{:S(2)}) copy-start(f32[3]{0:T(128)} %get-tuple-element.509) | copy-start | bytes 40 | tf_op jit(solution)/shard_map/while
  79.8 4.0 copy-start.7
  80.5 6.4 %copy-start.14 = (f32[3]{0:T(128)S(1)}, f32[3]{0:T(128)}, u32[]{:S(2)}) copy-start(f32[3]{0:T(128)} %get-tuple-element.509) | copy-start | bytes 40 | tf_op jit(solution)/shard_map/while
  113.9 4.0 copy-start.7
  114.6 6.4 %copy-start.14 = (f32[3]{0:T(128)S(1)}, f32[3]{0:T(128)}, u32[]{:S(2)}) copy-start(f32[3]{0:T(128)} %get-tuple-element.509) | copy-start | bytes 40 | tf_op jit(solution)/shard_map/while
  147.9 4.0 copy-start.7
  148.7 6.4 %copy-start.14 = (f32[3]{0:T(128)S(1)}, f32[3]{0:T(128)}, u32[]{:S(2)}) copy-start(f32[3]{0:T(128)} %get-tuple-element.509) | copy-start | bytes 40 | tf_op jit(solution)/shard_map/while
  182.0 4.0 copy-start.7
  182.7 6.4 %copy-start.14 = (f32[3]{0:T(128)S(1)}, f32[3]{0:T(128)}, u32[]{:S(2)}) copy-start(f32[3]{0:T(128)} %get-tuple-element.509) | copy-start | bytes 40 | tf_op jit(solution)/shard_map/while
  216.1 4.0 copy-start.7
  216.8 6.4 %copy-start.14 = (f32[3]{0:T(128)S(1)}, f32[3]{0:T(128)}, u32[]{:S(2)}) copy-start(f32[3]{0:T(128)} %get-tuple-element.509) | copy-start | bytes 40 | tf_op jit(solution)/shard_map/while
  250.1 4.0 copy-start.7
  250.8 6.4 %copy-start.14 = (f32[3]{0:T(128)S(1)}, f32[3]{0:T(128)}, u32[]{:S(2)}) copy-start(f32[3]{0:T(128)} %get-tuple-element.509) | copy-start | bytes 40 | tf_op jit(solution)/shard_map/while
  284.2 4.0 copy-start.7
  284.9 6.4 %copy-start.14 = (f32[3]{0:T(128)S(1)}, f32[3]{0:T(128)}, u32[]{:S(2)}) copy-start(f32[3]{0:T(128)} %get-tuple-element.509) | copy-start | bytes 40 | tf_op jit(solution)/shard_map/while
  318.2 4.0 copy-start.7
  318.9 6.4 %copy-start.14 = (f32[3]{0:T(128)S(1)}, f32[3]{0:T(128)}, u32[]{:S(2)}) copy-start(f32[3]{0:T(128)} %get-tuple-element.509) | copy-start | bytes 40 | tf_op jit(solution)/shard_map/while
  352.3 4.0 copy-start.7
  353.0 6.4 %copy-start.14 = (f32[3]{0:T(128)S(1)}, f32[3]{0:T(128)}, u32[]{:S(2)}) copy-start(f32[3]{0:T(128)} %get-tuple-element.509) | copy-start | bytes 40 | tf_op jit(solution)/shard_map/while
  386.3 4.0 copy-start.7
  387.1 6.4 %copy-start.14 = (f32[3]{0:T(128)S(1)}, f32[3]{0:T(128)}, u32[]{:S(2)}) copy-start(f32[3]{0:T(128)} %get-tuple-element.509) | copy-start | bytes 40 | tf_op jit(solution)/shard_map/while
  421.1 6.4 %copy-start.14 = (f32[3]{0:T(128)S(1)}, f32[3]{0:T(128)}, u32[]{:S(2)}) copy-start(f32[3]{0:T(128)} %get-tuple-element.509) | copy-start | bytes 40 | tf_op jit(solution)/shard_map/while
  427.5 43.2 %copy-start.5 = (f32[3,1536]{1,0:T(4,128)S(1)}, f32[3,1536]{1,0:T(4,128)}, u32[]{:S(2)}) copy-start(f32[3,1536]{1,0:T(4,128)} %param.17) | copy-start | bytes 55300
  427.5 43.2 %copy-start.12 = (f32[3,1536]{1,0:T(4,128)S(1)}, f32[3,1536]{1,0:T(4,128)}, u32[]{:S(2)}) copy-start(f32[3,1536]{1,0:T(4,128)} %param.18) | copy-start | bytes 55300
  427.5 43.2 %copy-start.16 = (f32[1536]{0:T(1024)S(1)}, f32[1536]{0:T(1024)}, u32[]{:S(2)}) copy-start(f32[1536]{0:T(1024)} %copy-done.15) | copy-start | bytes 18436
  460.2 6.8 %collective-permute-start.2 = (f32[24,192]{0,1:T(8,128)S(1)}, f32[24,192]{0,1:T(8,128)S(1)}, u32[]{:S(2)}, u32[]{:S(2)}) collective-permute-start(f32[24,192]{0,1:T(8,128)S(1)} %slice.250), channel_id=1, source_target_pairs={{0,1},{1,2},{2,3},{3,4},{4,5},{5,6},{6,7},{7,8},{8,9},{9,10},{10,1... | collective-permute-start | bytes 55304 | tf_op jit(solution)/shard_map/ppermute | solution.py:18
  462.3 6.8 %collective-permute-start.3 = (f32[24,96]{0,1:T(8,128)S(1)}, f32[24,96]{0,1:T(8,128)S(1)}, u32[]{:S(2)}, u32[]{:S(2)}) collective-permute-start(f32[24,96]{0,1:T(8,128)S(1)} %slice.251), channel_id=1, source_target_pairs={{0,2},{1,3},{2,4},{3,5},{4,6},{5,7},{6,8},{7,9},{8,10},{9,11},{10,... | collective-permute-start | bytes 27656 | tf_op jit(solution)/shard_map/ppermute | solution.py:18
  (102 other events, 189.2 us)
where the time goes:
time: 478 us; the launch traced here: 471 us
  local copies, waits for them, and re-layouts  263 us (55%)
  other arithmetic  127 us (27%)
  matrix products  30.1 us (6%)
  blocking collectives  29.8 us (6%)
  between operations  6.79 us (1%)
  waiting for transfers between devices  6.77 us (1%)
  starting transfers between devices  6.18 us (1%)
    slice x48, local copies, waits for them, and re-layouts, pair_tiles(): charge_pair = first_rows[3][:, None, :] * second_rows[3][None, :, :]  61.5 us
    slice x24, local copies, waits for them, and re-layouts, pair_tiles(): dispersion = first_rows[4][:, None, :] * second_rows[4][None, :, :]  40.2 us
    gather x12, local copies, waits for them, and re-layouts, pair_tiles(): jnp.take(slot_table, pair_rows[0], axis=0).T.reshape(6, 8, tile_width)  32.3 us
    gather x12, local copies, waits for them, and re-layouts, pair_tiles(): jnp.take(slot_table, pair_rows[1], axis=0).T.reshape(6, 8, tile_width)  32.3 us
    slice x24, local copies, waits for them, and re-layouts, pair_tiles(): delta_z = second_rows[2][None, :, :] - first_rows[2][:, None, :] + image_z  32 us
    dot_general x12, matrix products, one_block(): jnp.dot(selector, tile_terms, precision=lax.Precision.HIGHEST, preferred_...  30.1 us
    psum x1, blocking collectives, on_device(): overall_motion_work = lax.psum(kinetic, 'gx')  29.8 us
    add x12, other arithmetic, one_block(): return (accumulated, virial + partial_value)  25 us
  transfers between devices with their start and end apart: 4, of which 2 were waited for; matrix products, arithmetic and copies ran while one was open for 1% of the time, Pallas kernels for 0%

commit v1 on v0

--- a/solution.py
+++ b/solution.py
@@ -74,7 +74,8 @@
     axis_count = lax.axis_size("gx")
     inverse_mass = atom_params[3]
     kinetic = 0.5 * jnp.sum(velocities * velocities / inverse_mass[None, :], axis=1)
-    overall_motion_work = lax.psum(kinetic, "gx")
+    parts = lax.all_gather(kinetic, "gx", axis=0, tiled=False)
+    overall_motion_work = parts.sum(axis=0)
     packed = jnp.concatenate([positions, atom_params[:3]], axis=0)
     far_rows = packed.reshape(6, clusters, 8)[:, halo_far, :].reshape(6, far_clusters * 8)
     near_rows = passed_along(packed, "gx", -1)

time: 478 us -> 479 us (level)
    psum x1 -> x0, blocking collectives: 29.8 us -> none  [on_device(): overall_motion_work = lax.psum(kinetic, 'gx')]
    unnamed x0 -> x1, blocking collectives: none -> 29.8 us
where the time goes in v1:
time: 479 us; the launch traced here: 472 us
  local copies, waits for them, and re-layouts  263 us (55%)
  other arithmetic  126 us (26%)
  matrix products  30.1 us (6%)
  blocking collectives  29.8 us (6%)
  between operations  7.49 us (2%)
  waiting for transfers between devices  6.77 us (1%)
  starting transfers between devices  6.18 us (1%)
    slice x48, local copies, waits for them, and re-layouts, pair_tiles(): charge_pair = first_rows[3][:, None, :] * second_rows[3][None, :, :]  61.5 us
    slice x24, local copies, waits for them, and re-layouts, pair_tiles(): dispersion = first_rows[4][:, None, :] * second_rows[4][None, :, :]  40.2 us
    gather x12, local copies, waits for them, and re-layouts, pair_tiles(): jnp.take(slot_table, pair_rows[0], axis=0).T.reshape(6, 8, tile_width)  32.3 us
    gather x12, local copies, waits for them, and re-layouts, pair_tiles(): jnp.take(slot_table, pair_rows[1], axis=0).T.reshape(6, 8, tile_width)  32.3 us
    slice x24, local copies, waits for them, and re-layouts, pair_tiles(): delta_z = second_rows[2][None, :, :] - first_rows[2][:, None, :] + image_z  32 us
    dot_general x12, matrix products, one_block(): jnp.dot(selector, tile_terms, precision=lax.Precision.HIGHEST, preferred_...  30.1 us
    unnamed x1, blocking collectives  29.8 us
    add x12, other arithmetic, one_block(): return (accumulated, virial + partial_value)  25 us
  transfers between devices with their start and end apart: 4, of which 2 were waited for; matrix products, arithmetic and copies ran while one was open for 1% of the time, Pallas kernels for 0%

profile of v1, /device:TPU:0, one launch (start us, length us, event | category | flops | bytes accessed | tf_op | source)
XLA Modules:
  0.0 472.4 jit_solution(16696163150835289652)
XLA Ops:
  1.4 5.5 %collective-permute-start = (f32[6,1536]{1,0:T(8,128)S(1)}, f32[6,1536]{1,0:T(8,128)S(1)}, u32[]{:S(2)}, u32[]{:S(2)}) collective-permute-start(f32[6,1536]{1,0:T(8,128)S(1)} %pad_maximum_fusion.1), channel_id=1, source_target_pairs={{0,15},{1,0},{2,1},{3,2},{4,3},{5,4},{6,5},{7,6},{8,7},{9,8},{10,9... | collective-permute-start | bytes 110600 | tf_op jit(solution)/shard_map/ppermute | solution.py:18
  19.6 408.8 %while.18 = (s32[]{:T(128)}, f32[480,24]{0,1:T(8,128)}, f32[3]{0:T(128)}, s32[]{:T(128)}, s32[3,16896]{1,0:T(4,128)}, /*index=5*/s32[4,16896]{1,0:T(4,128)}, s32...) while((s32[]{:T(128)}, f32[480,24]{0,1:T(8,128)}, ...), condition=%wide.region_10.12_spmd.clone, body=%wide.region_0.11_spmd.clone.sunk | while | flops 397501280 | bytes 8990699 | solution.py:110
  26.8 2.7 gather_fusion.1
  29.8 2.7 gather_fusion
  60.9 2.7 gather_fusion.1
  63.8 2.7 gather_fusion
  95.0 2.7 gather_fusion.1
  97.9 2.7 gather_fusion
  129.0 2.7 gather_fusion.1
  132.0 2.7 gather_fusion
  163.1 2.7 gather_fusion.1
  166.1 2.7 gather_fusion
  186.8 2.5 fusion.65
  197.2 2.7 gather_fusion.1
  200.1 2.7 gather_fusion
  220.8 2.5 fusion.65
  231.2 2.7 gather_fusion.1
  234.2 2.7 gather_fusion
  265.3 2.7 gather_fusion.1
  268.2 2.7 gather_fusion
  289.0 2.5 fusion.65
  299.3 2.7 gather_fusion.1
  302.3 2.7 gather_fusion
  323.0 2.5 fusion.65
  333.4 2.7 gather_fusion.1
  336.3 2.7 gather_fusion
  367.4 2.7 gather_fusion.1
  370.4 2.7 gather_fusion
  401.5 2.7 gather_fusion.1
  404.5 2.7 gather_fusion
  428.3 29.8 %all-reduce.1 = (f32[48]{0:T(128)S(1)}, f32[3]{0:T(128)S(1)}) all-reduce(f32[48]{0:T(128)} %copy-done.21, f32[3]{0:T(128)} %get-tuple-element.496), channel_id=2, replica_groups=mesh['rep'=2,'gx'=16] {'gx'}, use_global_device_ids=true, to_apply=%add | all-reduce | flops 51 | bytes 408
  463.2 4.7 %collective-permute-done.2 = f32[24,192]{0,1:T(8,128)S(1)} collective-permute-done((f32[24,192]{0,1:T(8,128)S(1)}, f32[24,192]{0,1:T(8,128)S(1)}, u32[]{:S(2)}, u32[]{:S(2)}) %collective-permute-start.2) | collective-permute-done | bytes 18464 | tf_op jit(solution)/shard_map/ppermute | solution.py:18
  (785 shorter events, 348.0 us)
Async XLA Ops:
  1.4 15.4 %collective-permute-start = (f32[6,1536]{1,0:T(8,128)S(1)}, f32[6,1536]{1,0:T(8,128)S(1)}, u32[]{:S(2)}, u32[]{:S(2)}) collective-permute-start(f32[6,1536]{1,0:T(8,128)S(1)} %pad_maximum_fusion.1), channel_id=1, source_target_pairs={{0,15},{1,0},{2,1},{3,2},{4,3},{5,4},{6,5},{7,6},{8,7},{9,8},{10,9... | collective-permute-start | bytes 110600 | tf_op jit(solution)/shard_map/ppermute | solution.py:18
  8.5 8.4 %copy-start.4 = (f32[3,1536]{1,0:T(4,128)S(1)}, f32[3,1536]{1,0:T(4,128)}, u32[]{:S(2)}) copy-start(f32[3,1536]{1,0:T(4,128)} %param.17) | copy-start | bytes 55300
  9.8 6.8 %collective-permute-start.1 = (f32[6,768]{1,0:T(8,128)S(1)}, f32[6,768]{1,0:T(8,128)S(1)}, u32[]{:S(2)}, u32[]{:S(2)}) collective-permute-start(f32[6,768]{1,0:T(8,128)S(1)} %reshape.324), channel_id=1, source_target_pairs={{0,14},{1,15},{2,0},{3,1},{4,2},{5,3},{6,4},{7,5},{8,6},{9,7},{10,... | collective-permute-start | bytes 55304 | tf_op jit(solution)/shard_map/ppermute | solution.py:18
  10.5 6.3 %copy-start.15 = (f32[1536]{0:T(1024)}, f32[1536]{0:T(1024)S(1)}, u32[]{:S(2)}) copy-start(f32[1536]{0:T(1024)S(1)} %slice_reduce_fusion) | copy-start | bytes 18436
  12.0 4.6 copy-start.21
  46.5 4.0 copy-start.7
  47.2 6.4 %copy-start.14 = (f32[3]{0:T(128)S(1)}, f32[3]{0:T(128)}, u32[]{:S(2)}) copy-start(f32[3]{0:T(128)} %get-tuple-element.509) | copy-start | bytes 40 | tf_op jit(solution)/shard_map/while
  80.6 4.0 copy-start.7
  81.3 6.4 %copy-start.14 = (f32[3]{0:T(128)S(1)}, f32[3]{0:T(128)}, u32[]{:S(2)}) copy-start(f32[3]{0:T(128)} %get-tuple-element.509) | copy-start | bytes 40 | tf_op jit(solution)/shard_map/while
  114.7 4.0 copy-start.7
  115.4 6.4 %copy-start.14 = (f32[3]{0:T(128)S(1)}, f32[3]{0:T(128)}, u32[]{:S(2)}) copy-start(f32[3]{0:T(128)} %get-tuple-element.509) | copy-start | bytes 40 | tf_op jit(solution)/shard_map/while
  148.8 4.0 copy-start.7
  149.5 6.4 %copy-start.14 = (f32[3]{0:T(128)S(1)}, f32[3]{0:T(128)}, u32[]{:S(2)}) copy-start(f32[3]{0:T(128)} %get-tuple-element.509) | copy-start | bytes 40 | tf_op jit(solution)/shard_map/while
  182.8 4.0 copy-start.7
  183.5 6.4 %copy-start.14 = (f32[3]{0:T(128)S(1)}, f32[3]{0:T(128)}, u32[]{:S(2)}) copy-start(f32[3]{0:T(128)} %get-tuple-element.509) | copy-start | bytes 40 | tf_op jit(solution)/shard_map/while
  216.9 4.0 copy-start.7
  217.6 6.4 %copy-start.14 = (f32[3]{0:T(128)S(1)}, f32[3]{0:T(128)}, u32[]{:S(2)}) copy-start(f32[3]{0:T(128)} %get-tuple-element.509) | copy-start | bytes 40 | tf_op jit(solution)/shard_map/while
  250.9 4.0 copy-start.7
  251.7 6.4 %copy-start.14 = (f32[3]{0:T(128)S(1)}, f32[3]{0:T(128)}, u32[]{:S(2)}) copy-start(f32[3]{0:T(128)} %get-tuple-element.509) | copy-start | bytes 40 | tf_op jit(solution)/shard_map/while
  285.0 4.0 copy-start.7
  285.7 6.4 %copy-start.14 = (f32[3]{0:T(128)S(1)}, f32[3]{0:T(128)}, u32[]{:S(2)}) copy-start(f32[3]{0:T(128)} %get-tuple-element.509) | copy-start | bytes 40 | tf_op jit(solution)/shard_map/while
  319.0 4.0 copy-start.7
  319.8 6.4 %copy-start.14 = (f32[3]{0:T(128)S(1)}, f32[3]{0:T(128)}, u32[]{:S(2)}) copy-start(f32[3]{0:T(128)} %get-tuple-element.509) | copy-start | bytes 40 | tf_op jit(solution)/shard_map/while
  353.8 6.4 %copy-start.14 = (f32[3]{0:T(128)S(1)}, f32[3]{0:T(128)}, u32[]{:S(2)}) copy-start(f32[3]{0:T(128)} %get-tuple-element.509) | copy-start | bytes 40 | tf_op jit(solution)/shard_map/while
  387.2 4.0 copy-start.7
  387.9 6.4 %copy-start.14 = (f32[3]{0:T(128)S(1)}, f32[3]{0:T(128)}, u32[]{:S(2)}) copy-start(f32[3]{0:T(128)} %get-tuple-element.509) | copy-start | bytes 40 | tf_op jit(solution)/shard_map/while
  421.9 6.4 %copy-start.14 = (f32[3]{0:T(128)S(1)}, f32[3]{0:T(128)}, u32[]{:S(2)}) copy-start(f32[3]{0:T(128)} %get-tuple-element.509) | copy-start | bytes 40 | tf_op jit(solution)/shard_map/while
  428.3 43.3 %copy-start.5 = (f32[3,1536]{1,0:T(4,128)S(1)}, f32[3,1536]{1,0:T(4,128)}, u32[]{:S(2)}) copy-start(f32[3,1536]{1,0:T(4,128)} %param.17) | copy-start | bytes 55300
  428.3 43.3 %copy-start.12 = (f32[3,1536]{1,0:T(4,128)S(1)}, f32[3,1536]{1,0:T(4,128)}, u32[]{:S(2)}) copy-start(f32[3,1536]{1,0:T(4,128)} %param.18) | copy-start | bytes 55300
  428.3 43.3 %copy-start.16 = (f32[1536]{0:T(1024)S(1)}, f32[1536]{0:T(1024)}, u32[]{:S(2)}) copy-start(f32[1536]{0:T(1024)} %copy-done.15) | copy-start | bytes 18436
  461.1 6.8 %collective-permute-start.2 = (f32[24,192]{0,1:T(8,128)S(1)}, f32[24,192]{0,1:T(8,128)S(1)}, u32[]{:S(2)}, u32[]{:S(2)}) collective-permute-start(f32[24,192]{0,1:T(8,128)S(1)} %slice.250), channel_id=1, source_target_pairs={{0,1},{1,2},{2,3},{3,4},{4,5},{5,6},{6,7},{7,8},{8,9},{9,10},{10,1... | collective-permute-start | bytes 55304 | tf_op jit(solution)/shard_map/ppermute | solution.py:18
  463.2 6.8 %collective-permute-start.3 = (f32[24,96]{0,1:T(8,128)S(1)}, f32[24,96]{0,1:T(8,128)S(1)}, u32[]{:S(2)}, u32[]{:S(2)}) collective-permute-start(f32[24,96]{0,1:T(8,128)S(1)} %slice.251), channel_id=1, source_target_pairs={{0,2},{1,3},{2,4},{3,5},{4,6},{5,7},{6,8},{7,9},{8,10},{9,11},{10,... | collective-permute-start | bytes 27656 | tf_op jit(solution)/shard_map/ppermute | solution.py:18
  (104 other events, 197.2 us)
